TPU v7x, 32 devices: a whole 2x2x4 slice. The times are simulated.
32 devices in a mesh: gy: 16 (over z, y, core), gz: 2 (over x).
Axes of the slice: x: 2, y: 2, z: 4, core: 2. Of those that a mesh axis runs over, the one named last changes fastest.
Arguments:
- random_fields: bfloat16 [16, 3, 2048, 512], P(None, None, 'gy', 'gz'), may hold values from -6 to 6
- previous: float32 [3, 2048, 512], P(None, 'gy', 'gz'), may hold values from -6 to 6
- decay: float32 [3, 512], P(None, 'gz'), may hold values from 0.2 to 0.95
- mean_flow: float32 [3, 512], P(None, 'gz'), may hold values from 0 to 1.5
- lund_diag: float32 [3, 512], P(None, 'gz'), may hold values from 0.3 to 1.5
- lund_off: float32 [3, 512], P(None, 'gz'), may hold values from -0.6 to 0.6
Outputs:
- velocity: float32 [16, 3, 2048, 512], P(None, None, 'gy', 'gz')
All inputs are finite; a program needn't handle non-finite values.
Results may differ from a plain program's by a relative error of at most 0.0015.
The roundings to bfloat16 on the way count: a program that leaves them out, or rounds other values in their place, can miss the bound.
Values may be sent and summed in bfloat16 or wider, within the bound.
No kernel may reach another device: no remote copies, remote signals or barrier semaphores. Data moves between devices by JAX's collectives and lax.ppermute only.
A program may use at most 128 MiB of HBM per device.

v0:
```python
import functools
import math

import jax
import jax.numpy as jnp
from jax import lax
from jax.experimental import pallas as pl
from jax.experimental.pallas import tpu as pltpu
from jax.sharding import PartitionSpec as P

HALF = 96


VMEM = pl.BlockSpec(memory_space=pltpu.VMEM)
GRANT = 12 * 2**20


def pairs(count, first, closed):
    found = []
    for low in range(first, count, 2):
        if low + 1 < count or closed:
            high = (low + 1) % count
            found += [(low, high), (high, low)]
    return found


def chunks_of(steps):
    cut = lambda ends: [(a, b - a) for a, b in zip([0] + ends, ends)]
    sixteenths = lambda *parts: sorted({max(1, p * steps // 16) for p in parts})
    return cut(sixteenths(5, 11, 16)), cut(sixteenths(5, 10, 13, 15, 16))


def parity(axis):
    return lax.axis_index(axis) % 2


def half_of(block):
    odd = parity("gz")
    return odd if block else 1 - odd


def taps(lag):
    scale = HALF * 1.0
    offsets = lax.broadcasted_iota(jnp.int32, (8, 2 * HALF + 1), 1) - HALF
    offsets = offsets.astype(jnp.float32)
    kernel = jnp.exp(-math.pi * offsets * offsets / (2.0 * scale * scale))
    norm = jnp.sqrt(jnp.sum(kernel * kernel, axis=1, keepdims=True))[:1, :1]
    lag = lag.astype(jnp.float32)
    value = jnp.exp(-math.pi * lag * lag / (2.0 * scale * scale)) / norm
    return jnp.where(jnp.abs(lag) <= HALF, value, jnp.zeros_like(value)).astype(jnp.bfloat16)


def bands_kernel(weights, walls):
    rows = weights.shape[0]
    before, after = -HALF, rows
    odd = parity("gy")
    i = lax.broadcasted_iota(jnp.int32, weights.shape, 0)
    j = lax.broadcasted_iota(jnp.int32, weights.shape, 1)
    at_core = j + jnp.where(odd == 1, before, after)
    at_link = j - HALF - rows + jnp.where(odd == 1, after, before)
    at = jnp.where(j < HALF, at_core, jnp.where(j < HALF + rows, j - HALF, at_link))
    weights[...] = taps(at - i)

    cols = walls.shape[1]
    lanes = cols // 2
    odd = parity("gz")
    j = lax.broadcasted_iota(jnp.int32, walls.shape, 0)
    m = lax.broadcasted_iota(jnp.int32, walls.shape, 1)
    at_far = j + half_of(1) * lanes
    at_near = j - lanes + half_of(0) * lanes
    at_near_halo = j - cols + jnp.where(odd == 1, -HALF, cols)
    at_far_halo = j - cols - HALF + jnp.where(odd == 1, cols, -HALF)
    at = jnp.where(j < cols + HALF, at_near_halo, at_far_halo)
    at = jnp.where(j < lanes, at_far, jnp.where(j < cols, at_near, at))
    walls[...] = taps(at - m)


def pack_kernel(cuts, own, *outs):
    rows = own.shape[2]
    for (start, count, side, block), out in zip(cuts, outs):
        lanes = out.shape[3]
        odd = parity("gy")
        row = pl.multiple_of((1 - odd if side else odd) * (rows - HALF), math.gcd(rows - HALF, 128))
        lane = pl.multiple_of(half_of(block) * lanes, lanes)
        for t in range(count):
            for c in range(own.shape[1]):
                out[t, c] = own[start + t, c, pl.ds(row, HALF), pl.ds(lane, lanes)]


def span_product(weights, core, own, link):
    planes = [jnp.concatenate([core[p], own[p], link[p]], axis=0) for p in range(len(own))]
    return jnp.dot(weights, jnp.concatenate(planes, axis=1), preferred_element_type=jnp.float32)


def smooth_planes(block, start, first, count, weights, own, core, link):
    parts, lanes = own.shape[1], core.shape[3]
    lane = pl.multiple_of(half_of(block) * lanes, lanes)
    index = [(t, c) for t in range(count) for c in range(parts)]
    product = span_product(
        weights[...],
        [core[start + first + t, c] for t, c in index],
        [own[start + first + t, c, :, pl.ds(lane, lanes)] for t, c in index],
        [link[first + t, c] for t, c in index],
    ).astype(own.dtype)
    return {i: product[:, p * lanes : (p + 1) * lanes] for p, i in enumerate(index)}


def smooth_kernel(start, block, per, weights, own, core, link, out, edge):
    steps = out.shape[0]
    width = edge.shape[2]
    for first in range(0, steps, per):
        planes = smooth_planes(block, start, first, min(per, steps - first), weights, own, core, link)
        upper = half_of(block)
        for (t, c), plane in planes.items():
            out[first + t, c] = plane
        turned = {i: plane.T for i, plane in planes.items()}

        @pl.when(upper == 1)
        def _():
            for (t, c), plane in turned.items():
                edge[first + t, c] = plane[plane.shape[0] - width :, :]

        @pl.when(upper == 0)
        def _():
            for (t, c), plane in turned.items():
                edge[first + t, c] = plane[:width, :]


def velocity_kernel(chunk, sources, raw, halos, kept, keeps, last, *refs):
    start, count = chunk
    (weights, walls, decay, mean, diag, off, before, own, core, link), rest = refs[:10], refs[10:]
    near, rest = rest[: len(sources)], rest[len(sources) :]
    near_halo, rest = (rest[: len(sources)], rest[len(sources) :]) if halos[0] else ((), rest)
    far_halo, rest = (rest[:1], rest[1:]) if halos[1] else ((), rest)
    kept_ref, rest = (rest[0], rest[1:]) if kept else (None, rest)
    if keeps:
        state, out = rest[-2:]
    elif last:
        velocity, out, sems = rest[-3:]
    else:
        velocity, state, out, sems = rest[-4:]
    copies = []
    if kept:
        copies.append(pltpu.make_async_copy(kept_ref, velocity.at[pl.ds(*kept)], sems.at[0]))
        copies[0].start()

    parts, rows = own.shape[1:3]
    keep = decay[...]
    fresh = jnp.sqrt(1.0 - keep * keep)
    line = lambda x, c: x[c : c + 1, :]
    u, d, o = mean[...], diag[...], off[...]
    band = walls[...]
    now = [before[c] for c in range(parts)]
    for first in range(0, count, 2):
        group = range(first, min(first + 2, count))
        if raw:
            far = smooth_planes(1, start, first, len(group), weights, own, core, link)
        for t in group:
            step = start + t
            q = max(q for q, at in enumerate(sources) if at <= step)
            cells = []
            for c in range(parts):
                row = [far[t - first, c] if raw else own[t, c], near[q][step - sources[q], c]]
                row += [ref[step - sources[q], c].T for ref in near_halo[q : q + 1]]
                row += [ref[t, c].T for ref in far_halo]
                cells.append(jnp.concatenate(row, axis=1))
            filtered = jnp.dot(jnp.concatenate(cells, axis=0), band, preferred_element_type=jnp.float32)
            for c in range(parts):
                now[c] = line(keep, c) * now[c] + line(fresh, c) * filtered[c * rows : (c + 1) * rows]
                value = line(u, c) + line(d, c) * now[c]
                for e in range(c):
                    value = value + line(o, (c * (c - 1)) // 2 + e) * now[e]
                out[t, c] = value
                if not keeps:
                    k = bool(kept) + t * parts + c
                    copies.append(pltpu.make_async_copy(out.at[t, c], velocity.at[step, c], sems.at[k]))
                    copies[-1].start()
    if not last:
        for c in range(parts):
            state[c] = now[c]
    for copy in copies:
        copy.wait()


def shards(random_fields, previous, decay, mean_flow, lund_diag, lund_off):
    steps, parts, rows, cols = random_fields.shape
    lanes = cols // 2
    span_count = lax.axis_size("gy")
    wall_count = lax.axis_size("gz")
    kind = random_fields.dtype
    params = pltpu.CompilerParams(vmem_limit_bytes=GRANT)

    core_pairs = pairs(span_count, 0, True)
    link_pairs = pairs(span_count, 1, True)
    near_pairs = pairs(wall_count, 0, False)
    far_pairs = pairs(wall_count, 1, False)
    near_chunks, far_chunks = chunks_of(steps)

    start, count = near_chunks[0]
    first_cut = lax.dynamic_slice(
        random_fields,
        (start, 0, parity("gy") * (rows - HALF), half_of(0) * lanes),
        (count, parts, HALF, lanes),
    )
    own, first_cut = lax.optimization_barrier((random_fields, first_cut))

    cuts = [(0, steps, 1, 0)] + [(s, n, 0, 0) for s, n in near_chunks[1:]]
    cuts += [(s, n, 0, 1) for s, n in far_chunks] + [(0, steps, 1, 1)]
    packed = pl.pallas_call(
        functools.partial(pack_kernel, cuts),
        out_shape=[jax.ShapeDtypeStruct((n, parts, HALF, lanes), kind) for _, n, _, _ in cuts],
        in_specs=[VMEM],
        out_specs=[VMEM] * len(cuts),
        compiler_params=params,
        name="pack",
    )(own)
    near_core = lax.ppermute(packed[0], "gy", core_pairs)
    far_core = lax.ppermute(packed[-1], "gy", core_pairs)
    links = [lax.ppermute(x, "gy", link_pairs) for x in [first_cut, *packed[1:-1]]]
    near_link, far_link = links[: len(near_chunks)], links[len(near_chunks) :]

    depth = cols + HALF * (bool(near_pairs) + bool(far_pairs))
    weights, walls = pl.pallas_call(
        bands_kernel,
        out_shape=(
            jax.ShapeDtypeStruct((rows, rows + 2 * HALF), kind),
            jax.ShapeDtypeStruct((depth, cols), kind),
        ),
        out_specs=(VMEM, VMEM),
        compiler_params=params,
        name="bands",
    )()

    def smooth(start, count, block, core, link):
        return pl.pallas_call(
            functools.partial(smooth_kernel, start, block, 2),
            out_shape=(
                jax.ShapeDtypeStruct((count, parts, rows, lanes), kind),
                jax.ShapeDtypeStruct((count, parts, HALF, rows), kind),
            ),
            in_specs=[VMEM] * 4,
            out_specs=(VMEM, VMEM),
            compiler_params=params,
            cost_estimate=pl.CostEstimate(
                flops=2 * count * parts * rows * lanes * (rows + 2 * HALF),
                bytes_accessed=4 * count * parts * lanes * (rows + HALF),
                transcendentals=0,
            ),
            name="smooth",
        )(weights, own, core, link)

    near = [smooth(s, n, 0, near_core, link) for (s, n), link in zip(near_chunks, near_link)]
    near_halo, far_halo, far = [], [], None
    if near_pairs:
        near_halo = [lax.ppermute(edge, "gz", near_pairs) for _, edge in near]
    if far_pairs:
        far = [smooth(s, n, 1, far_core, link) for (s, n), link in zip(far_chunks, far_link)]
        far_halo = [lax.ppermute(edge, "gz", far_pairs) for _, edge in far]

    hbm = pl.BlockSpec(memory_space=pl.ANY)
    velocity, state, kept = None, previous, None
    for k, (s, n) in enumerate(far_chunks):
        last = k == len(far_chunks) - 1
        keeps = k == len(far_chunks) - 2
        used = [q for q, (at, count) in enumerate(near_chunks) if at < s + n and s < at + count]
        operands = [weights, walls, decay, mean_flow, lund_diag, lund_off, state]
        operands += [own if far is None else far[k][0], far_core, far_link[k]]
        operands += [near[q][0] for q in used] + ([near_halo[q] for q in used] if near_halo else []) + far_halo[k : k + 1]
        operands += [out] if kept else []
        specs = [VMEM] * len(operands)
        aliases = {}
        held = jax.ShapeDtypeStruct((n, parts, rows, cols), jnp.float32)
        shapes, places, scratch = [], [], []
        if not keeps:
            if velocity is not None:
                aliases = {len(operands): 0}
                operands.append(velocity)
                specs.append(hbm)
            shapes.append(jax.ShapeDtypeStruct((steps, parts, rows, cols), jnp.float32))
            places.append(hbm)
            scratch.append(pltpu.VMEM(held.shape, held.dtype))
            scratch.append(pltpu.SemaphoreType.DMA((bool(kept) + n * parts,)))
        if not last:
            shapes.append(jax.ShapeDtypeStruct(previous.shape, jnp.float32))
            places.append(VMEM)
        if keeps:
            shapes.append(held)
            places.append(VMEM)
        made = pl.pallas_call(
            functools.partial(
                velocity_kernel,
                (s, n),
                [near_chunks[q][0] for q in used],
                far is None,
                (bool(near_halo), bool(far_halo)),
                kept,
                keeps,
                last,
            ),
            out_shape=shapes,
            in_specs=specs,
            out_specs=places,
            scratch_shapes=scratch,
            input_output_aliases=aliases,
            compiler_params=params,
            cost_estimate=pl.CostEstimate(
                flops=2 * n * parts * rows * (lanes * (rows + 2 * HALF) + cols * depth),
                bytes_accessed=n * parts * rows * (4 * cols + 10 * lanes),
                transcendentals=0,
            ),
            name="velocity",
        )(*operands)
        if keeps:
            state, out = made
        elif last:
            (velocity,) = made
        else:
            velocity, state = made
        kept = (s, n) if keeps else None
    return velocity


def solution(mesh):
    return jax.shard_map(
        shards,
        mesh=mesh,
        in_specs=(
            P(None, None, "gy", "gz"),
            P(None, "gy", "gz"),
            P(None, "gz"),
            P(None, "gz"),
            P(None, "gz"),
            P(None, "gz"),
        ),
        out_specs=P(None, None, "gy", "gz"),
        check_vma=False,
    )
```

profile of v0, /device:TPU:1, one launch (start us, length us, event | category | flops | bytes accessed | tf_op | source)
XLA Modules:
  0.0 63.1 jit_solution(3401146364339632481)
XLA Ops:
  0.0 1.0 %constant_dynamic-slice_fusion = bf16[5,3,96,128]{3,2,1,0:T(8,128)(2,1)S(1)} fusion(bf16[16,3,128,256]{3,2,1,0:T(8,128)(2,1)} %refs_7_.4, s32[]{:T(128)S(6)} %select_n.18, s32[]{:T(128)S(6)} %select_n.20), kind=kLoop, calls=%fused_computation | loop fusion | bytes 737288 | tf_op jit(solution)/shard_map/dynamic_slice | solution.py:200
  1.0 0.0 copy-start
  1.0 1.9 %copy-done = bf16[16,3,128,256]{3,2,1,0:T(8,128)(2,1)S(1)} copy-done((bf16[16,3,128,256]{3,2,1,0:T(8,128)(2,1)S(1)}, bf16[16,3,128,256]{3,2,1,0:T(8,128)(2,1)}, u32[]{:S(2)}) %copy-start) | copy-done | bytes 3145752
  2.9 0.0 copy-start.1
  2.9 0.7 %pack.1 = (bf16[16,3,96,128]{3,2,1,0:T(8,128)(2,1)S(1)}, bf16[6,3,96,128]{3,2,1,0:T(8,128)(2,1)S(1)}, bf16[5,3,96,128]{3,2,1,0:T(8,128)(2,1)S(1)}, bf16[5,3,96,1...) custom-call(bf16[16,3,128,256]{3,2,1,0:T(8,128)(2,1)S(1)} %copy-done), custom_call_target="tpu_custom_call" | custom-call | tf_op jit(solution)/shard_map/pack/pallas_call | solution.py:209
  3.7 0.1 collective-permute-start.2
  3.7 0.5 collective-permute-start
  4.2 2.6 %collective-permute-start.6 = (bf16[6,3,96,128]{3,2,1,0:T(8,128)(2,1)S(1)}, bf16[6,3,96,128]{3,2,1,0:T(8,128)(2,1)S(1)}, u32[]{:S(2)}, u32[]{:S(2)}) collective-permute-start(bf16[6,3,96,128]{3,2,1,0:T(8,128)(2,1)S(1)} %get-tuple-element.43), channel_id=1, source_target_pairs={{2,4},{4,2},{6,8},{8,6},{10,12},{12,10},{14,16},{16,14},{18,20},{2... | collective-permute-start | bytes 1327112 | tf_op jit(solution)/shard_map/ppermute | solution.py:219
  6.9 0.0 collective-permute-start.3
  6.9 1.7 %collective-permute-start.9 = (bf16[5,3,96,128]{3,2,1,0:T(8,128)(2,1)S(1)}, bf16[5,3,96,128]{3,2,1,0:T(8,128)(2,1)S(1)}, u32[]{:S(2)}, u32[]{:S(2)}) collective-permute-start(bf16[5,3,96,128]{3,2,1,0:T(8,128)(2,1)S(1)} %get-tuple-element.49), channel_id=1, source_target_pairs={{2,4},{4,2},{6,8},{8,6},{10,12},{12,10},{14,16},{16,14},{18,20},{2... | collective-permute-start | bytes 1105928 | tf_op jit(solution)/shard_map/ppermute | solution.py:219
  8.6 28.8 %collective-permute-done.6.link = bf16[6,3,96,128]{3,2,1,0:T(8,128)(2,1)S(1)} collective-permute-done((bf16[6,3,96,128]{3,2,1,0:T(8,128)(2,1)S(1)}, bf16[6,3,96,128]{3,2,1,0:T(8,128)(2,1)S(1)}, u32[]{:S(2)}, u32[]{:S(2)}) %collective-permute-start.6) | collective-permute-done | bytes 442400 | tf_op jit(solution)/shard_map/ppermute | solution.py:219
  37.4 2.5 %collective-permute-start.1 = (bf16[5,3,96,128]{3,2,1,0:T(8,128)(2,1)S(1)}, bf16[5,3,96,128]{3,2,1,0:T(8,128)(2,1)S(1)}, u32[]{:S(2)}, u32[]{:S(2)}) collective-permute-start(bf16[5,3,96,128]{3,2,1,0:T(8,128)(2,1)S(1)} %get-tuple-element.36), channel_id=1, source_target_pairs={{2,4},{4,2},{6,8},{8,6},{10,12},{12,10},{14,16},{16,14},{18,20},{2... | collective-permute-start | bytes 1105928 | tf_op jit(solution)/shard_map/ppermute | solution.py:219
  39.9 0.4 bands.1
  40.2 0.0 collective-permute-done.2.core
  40.2 0.0 copy-done.1
  40.3 1.1 %smooth.4 = (bf16[6,3,128,128]{3,2,1,0:T(8,128)(2,1)S(1)}, bf16[6,3,96,128]{3,2,1,0:T(8,128)(2,1)S(1)}) custom-call(bf16[128,320]{1,0:T(8,128)(2,1)S(1)} %get-tuple-element.32.weights.refs_0_, bf16[16,3,128,256]{3,2,1,0:T(8,128)(2,1)S(1)} %copy-done.1, bf16[16,3,96,128]{3,2,1,0:T(8,128)(2,1)S(1)} %collective-permute-done.2.core, ...), custom_call_target="tpu_custom_call" | custom-call | flops 188743680 | bytes 2064384 | tf_op jit(solution)/shard_map/smooth/pallas_call | solution.py:235
  41.3 1.3 %collective-permute-start.7 = (bf16[6,3,96,128]{3,2,1,0:T(8,128)(2,1)S(1)}, bf16[6,3,96,128]{3,2,1,0:T(8,128)(2,1)S(1)}, u32[]{:S(2)}, u32[]{:S(2)}) collective-permute-start(bf16[6,3,96,128]{3,2,1,0:T(8,128)(2,1)S(1)} %get-tuple-element.45), channel_id=1, source_target_pairs={{0,1},{1,0},{2,3},{3,2},{4,5},{5,4},{6,7},{7,6},{8,9},{9,8},{10,11... | collective-permute-start | bytes 1327112 | tf_op jit(solution)/shard_map/ppermute | solution.py:255
  42.6 0.0 collective-permute-done.3.link
  42.6 1.0 %smooth.3 = (bf16[5,3,128,128]{3,2,1,0:T(8,128)(2,1)S(1)}, bf16[5,3,96,128]{3,2,1,0:T(8,128)(2,1)S(1)}) custom-call(bf16[128,320]{1,0:T(8,128)(2,1)S(1)} %get-tuple-element.32.weights.refs_0_, bf16[16,3,128,256]{3,2,1,0:T(8,128)(2,1)S(1)} %copy-done.1, bf16[16,3,96,128]{3,2,1,0:T(8,128)(2,1)S(1)} %collective-permute-done.2.core, ...), custom_call_target="tpu_custom_call" | custom-call | flops 157286400 | bytes 1720320 | tf_op jit(solution)/shard_map/smooth/pallas_call | solution.py:235
  43.6 0.0 copy-start.2
  43.6 0.0 copy-start.3
  43.7 0.0 copy-start.4
  43.7 0.0 copy-start.5
  43.7 0.0 copy-start.6
  43.7 0.4 collective-permute-start.4
  44.1 1.9 %collective-permute-done.9.link = bf16[5,3,96,128]{3,2,1,0:T(8,128)(2,1)S(1)} collective-permute-done((bf16[5,3,96,128]{3,2,1,0:T(8,128)(2,1)S(1)}, bf16[5,3,96,128]{3,2,1,0:T(8,128)(2,1)S(1)}, u32[]{:S(2)}, u32[]{:S(2)}) %collective-permute-start.9) | collective-permute-done | bytes 368672 | tf_op jit(solution)/shard_map/ppermute | solution.py:219
  46.0 1.7 %collective-permute-start.5 = (bf16[5,3,96,128]{3,2,1,0:T(8,128)(2,1)S(1)}, bf16[5,3,96,128]{3,2,1,0:T(8,128)(2,1)S(1)}, u32[]{:S(2)}, u32[]{:S(2)}) collective-permute-start(bf16[5,3,96,128]{3,2,1,0:T(8,128)(2,1)S(1)} %get-tuple-element.42), channel_id=1, source_target_pairs={{2,4},{4,2},{6,8},{8,6},{10,12},{12,10},{14,16},{16,14},{18,20},{2... | collective-permute-start | bytes 1105928 | tf_op jit(solution)/shard_map/ppermute | solution.py:219
  47.8 1.0 %smooth.5 = (bf16[5,3,128,128]{3,2,1,0:T(8,128)(2,1)S(1)}, bf16[5,3,96,128]{3,2,1,0:T(8,128)(2,1)S(1)}) custom-call(bf16[128,320]{1,0:T(8,128)(2,1)S(1)} %get-tuple-element.32.weights.refs_0_, bf16[16,3,128,256]{3,2,1,0:T(8,128)(2,1)S(1)} %copy-done.1, bf16[16,3,96,128]{3,2,1,0:T(8,128)(2,1)S(1)} %collective-permute-done.2.core, ...), custom_call_target="tpu_custom_call" | custom-call | flops 157286400 | bytes 1720320 | tf_op jit(solution)/shard_map/smooth/pallas_call | solution.py:235
  48.8 1.2 %collective-permute-done.1.refs_9_ = bf16[5,3,96,128]{3,2,1,0:T(8,128)(2,1)S(1)} collective-permute-done((bf16[5,3,96,128]{3,2,1,0:T(8,128)(2,1)S(1)}, bf16[5,3,96,128]{3,2,1,0:T(8,128)(2,1)S(1)}, u32[]{:S(2)}, u32[]{:S(2)}) %collective-permute-start.1) | collective-permute-done | bytes 368672 | tf_op jit(solution)/shard_map/ppermute | solution.py:219
  50.0 1.4 %collective-permute-start.10 = (bf16[5,3,96,128]{3,2,1,0:T(8,128)(2,1)S(1)}, bf16[5,3,96,128]{3,2,1,0:T(8,128)(2,1)S(1)}, u32[]{:S(2)}, u32[]{:S(2)}) collective-permute-start(bf16[5,3,96,128]{3,2,1,0:T(8,128)(2,1)S(1)} %get-tuple-element.51), channel_id=1, source_target_pairs={{0,1},{1,0},{2,3},{3,2},{4,5},{5,4},{6,7},{7,6},{8,9},{9,8},{10,11... | collective-permute-start | bytes 1105928 | tf_op jit(solution)/shard_map/ppermute | solution.py:255
  51.4 0.0 collective-permute-done.refs_8_
  51.4 1.8 %collective-permute-start.8 = (bf16[3,3,96,128]{3,2,1,0:T(8,128)(2,1)S(1)}, bf16[3,3,96,128]{3,2,1,0:T(8,128)(2,1)S(1)}, u32[]{:S(2)}, u32[]{:S(2)}) collective-permute-start(bf16[3,3,96,128]{3,2,1,0:T(8,128)(2,1)S(1)} %get-tuple-element.48), channel_id=1, source_target_pairs={{2,4},{4,2},{6,8},{8,6},{10,12},{12,10},{14,16},{16,14},{18,20},{2... | collective-permute-start | bytes 663560 | tf_op jit(solution)/shard_map/ppermute | solution.py:219
  53.2 0.0 collective-permute-done.4.refs_11_
  53.2 0.4 collective-permute-start.11
  53.6 0.0 copy-done.2
  53.6 0.0 copy-done.3
  53.6 0.0 copy-done.4
  53.6 0.0 copy-done.5
  53.7 0.0 copy-done.6
  53.7 2.2 %velocity.5 = (f32[16,3,128,256]{3,2,1,0:T(8,128)}, f32[3,128,256]{2,1,0:T(8,128)S(1)}) custom-call(bf16[128,320]{1,0:T(8,128)(2,1)S(1)} %get-tuple-element.32.weights.refs_0_, bf16[352,256]{1,0:T(8,128)(2,1)S(1)} %get-tuple-element.33.refs_1_, f32[3,256]{1,0:T(4,128)S(1)} %copy-done.3, f32[3,256]{1,0:T(4,128)S(1)} %copy-done.4, f32[3,256]{1,0:T(4,128)S(1)} %copy-done.5, ...), custom_call_target="tpu_custom_call" | custom-call | flops 503316480 | bytes 4423680 | tf_op jit(solution)/shard_map/velocity/pallas_call | solution.py:289
  55.9 0.0 collective-permute-done.5.refs_9_
  55.9 1.4 %collective-permute-start.12 = (bf16[1,3,96,128]{3,2,1,0:T(8,128)(2,1)S(1)}, bf16[1,3,96,128]{3,2,1,0:T(8,128)(2,1)S(1)}, u32[]{:S(2)}, u32[]{:S(2)}) collective-permute-start(bf16[1,3,96,128]{3,2,1,0:T(8,128)(2,1)S(1)} %get-tuple-element.56), channel_id=1, source_target_pairs={{2,4},{4,2},{6,8},{8,6},{10,12},{12,10},{14,16},{16,14},{18,20},{2... | collective-permute-start | bytes 221192 | tf_op jit(solution)/shard_map/ppermute | solution.py:219
  57.3 0.0 collective-permute-done.7.refs_11_.refs_12_
  57.3 2.2 %velocity.6 = (f32[16,3,128,256]{3,2,1,0:T(8,128)}, f32[3,128,256]{2,1,0:T(8,128)S(1)}) custom-call(bf16[128,320]{1,0:T(8,128)(2,1)S(1)} %get-tuple-element.32.weights.refs_0_, bf16[352,256]{1,0:T(8,128)(2,1)S(1)} %get-tuple-element.33.refs_1_, f32[3,256]{1,0:T(4,128)S(1)} %copy-done.3, f32[3,256]{1,0:T(4,128)S(1)} %copy-done.4, ...), custom_call_target="tpu_custom_call", output_to_operand_aliasing={{0}: (12, {})} | custom-call | flops 503316480 | bytes 4423680 | tf_op jit(solution)/shard_map/velocity/pallas_call | solution.py:289
  59.6 0.0 collective-permute-done.8.refs_9_
  59.6 0.0 collective-permute-done.10.refs_13_.refs_11_
  59.6 1.7 %velocity.7 = (f32[16,3,128,256]{3,2,1,0:T(8,128)}, f32[3,128,256]{2,1,0:T(8,128)S(1)}) custom-call(bf16[128,320]{1,0:T(8,128)(2,1)S(1)} %get-tuple-element.32.weights.refs_0_, bf16[352,256]{1,0:T(8,128)(2,1)S(1)} %get-tuple-element.33.refs_1_, f32[3,256]{1,0:T(4,128)S(1)} %copy-done.3, f32[3,256]{1,0:T(4,128)S(1)} %copy-done.4, ...), custom_call_target="tpu_custom_call", output_to_operand_aliasing={{0}: (14, {})} | custom-call | flops 301989888 | bytes 2654208 | tf_op jit(solution)/shard_map/velocity/pallas_call | solution.py:289
  61.3 0.0 collective-permute-done.11.refs_9_
  61.3 0.6 velocity.8
  61.9 0.0 collective-permute-done.12.refs_9_
  61.9 1.1 %velocity.9 = f32[16,3,128,256]{3,2,1,0:T(8,128)} custom-call(bf16[128,320]{1,0:T(8,128)(2,1)S(1)} %get-tuple-element.32.weights.refs_0_, bf16[352,256]{1,0:T(8,128)(2,1)S(1)} %get-tuple-element.33.refs_1_, f32[3,256]{1,0:T(4,128)S(1)} %copy-done.3, f32[3,256]{1,0:T(4,128)S(1)} %copy-done.4, ...), custom_call_target="tpu_custom_call", output_to_operand_aliasing={{}: (13, {})} | custom-call | flops 100663296 | bytes 884736 | tf_op jit(solution)/shard_map/velocity/pallas_call | solution.py:289
Async XLA Ops:
  1.0 1.9 %copy-start = (bf16[16,3,128,256]{3,2,1,0:T(8,128)(2,1)S(1)}, bf16[16,3,128,256]{3,2,1,0:T(8,128)(2,1)}, u32[]{:S(2)}) copy-start(bf16[16,3,128,256]{3,2,1,0:T(8,128)(2,1)} %refs_7_.4) | copy-start | bytes 9437188
  2.9 37.3 %copy-start.1 = (bf16[16,3,128,256]{3,2,1,0:T(8,128)(2,1)S(1)}, bf16[16,3,128,256]{3,2,1,0:T(8,128)(2,1)}, u32[]{:S(2)}) copy-start(bf16[16,3,128,256]{3,2,1,0:T(8,128)(2,1)} %refs_7_.4) | copy-start | bytes 9437188
  3.7 36.6 %collective-permute-start.2 = (bf16[16,3,96,128]{3,2,1,0:T(8,128)(2,1)S(1)}, bf16[16,3,96,128]{3,2,1,0:T(8,128)(2,1)S(1)}, u32[]{:S(2)}, u32[]{:S(2)}) collective-permute-start(bf16[16,3,96,128]{3,2,1,0:T(8,128)(2,1)S(1)} %get-tuple-element.37), channel_id=1, source_target_pairs={{0,2},{2,0},{4,6},{6,4},{8,10},{10,8},{12,14},{14,12},{16,18},{18,... | collective-permute-start | bytes 3538952 | tf_op jit(solution)/shard_map/ppermute | solution.py:217
  3.7 47.6 %collective-permute-start = (bf16[16,3,96,128]{3,2,1,0:T(8,128)(2,1)S(1)}, bf16[16,3,96,128]{3,2,1,0:T(8,128)(2,1)S(1)}, u32[]{:S(2)}, u32[]{:S(2)}) collective-permute-start(bf16[16,3,96,128]{3,2,1,0:T(8,128)(2,1)S(1)} %get-tuple-element.35), channel_id=1, source_target_pairs={{0,2},{2,0},{4,6},{6,4},{8,10},{10,8},{12,14},{14,12},{16,18},{18,... | collective-permute-start | bytes 3538952 | tf_op jit(solution)/shard_map/ppermute | solution.py:218
  4.2 33.1 %collective-permute-start.6 = (bf16[6,3,96,128]{3,2,1,0:T(8,128)(2,1)S(1)}, bf16[6,3,96,128]{3,2,1,0:T(8,128)(2,1)S(1)}, u32[]{:S(2)}, u32[]{:S(2)}) collective-permute-start(bf16[6,3,96,128]{3,2,1,0:T(8,128)(2,1)S(1)} %get-tuple-element.43), channel_id=1, source_target_pairs={{2,4},{4,2},{6,8},{8,6},{10,12},{12,10},{14,16},{16,14},{18,20},{2... | collective-permute-start | bytes 1327112 | tf_op jit(solution)/shard_map/ppermute | solution.py:219
  6.9 35.8 %collective-permute-start.3 = (bf16[5,3,96,128]{3,2,1,0:T(8,128)(2,1)S(1)}, bf16[5,3,96,128]{3,2,1,0:T(8,128)(2,1)S(1)}, u32[]{:S(2)}, u32[]{:S(2)}) collective-permute-start(bf16[5,3,96,128]{3,2,1,0:T(8,128)(2,1)S(1)} %constant_dynamic-slice_fusion), channel_id=1, source_target_pairs={{2,4},{4,2},{6,8},{8,6},{10,12},{12,10},{14,16},{16,14},{18,20},{2... | collective-permute-start | bytes 1105928 | tf_op jit(solution)/shard_map/ppermute | solution.py:219
  6.9 39.1 %collective-permute-start.9 = (bf16[5,3,96,128]{3,2,1,0:T(8,128)(2,1)S(1)}, bf16[5,3,96,128]{3,2,1,0:T(8,128)(2,1)S(1)}, u32[]{:S(2)}, u32[]{:S(2)}) collective-permute-start(bf16[5,3,96,128]{3,2,1,0:T(8,128)(2,1)S(1)} %get-tuple-element.49), channel_id=1, source_target_pairs={{2,4},{4,2},{6,8},{8,6},{10,12},{12,10},{14,16},{16,14},{18,20},{2... | collective-permute-start | bytes 1105928 | tf_op jit(solution)/shard_map/ppermute | solution.py:219
  37.4 12.6 %collective-permute-start.1 = (bf16[5,3,96,128]{3,2,1,0:T(8,128)(2,1)S(1)}, bf16[5,3,96,128]{3,2,1,0:T(8,128)(2,1)S(1)}, u32[]{:S(2)}, u32[]{:S(2)}) collective-permute-start(bf16[5,3,96,128]{3,2,1,0:T(8,128)(2,1)S(1)} %get-tuple-element.36), channel_id=1, source_target_pairs={{2,4},{4,2},{6,8},{8,6},{10,12},{12,10},{14,16},{16,14},{18,20},{2... | collective-permute-start | bytes 1105928 | tf_op jit(solution)/shard_map/ppermute | solution.py:219
  41.3 16.0 %collective-permute-start.7 = (bf16[6,3,96,128]{3,2,1,0:T(8,128)(2,1)S(1)}, bf16[6,3,96,128]{3,2,1,0:T(8,128)(2,1)S(1)}, u32[]{:S(2)}, u32[]{:S(2)}) collective-permute-start(bf16[6,3,96,128]{3,2,1,0:T(8,128)(2,1)S(1)} %get-tuple-element.45), channel_id=1, source_target_pairs={{0,1},{1,0},{2,3},{3,2},{4,5},{5,4},{6,7},{7,6},{8,9},{9,8},{10,11... | collective-permute-start | bytes 1327112 | tf_op jit(solution)/shard_map/ppermute | solution.py:255
  43.6 10.0 %copy-start.2 = (f32[3,128,256]{2,1,0:T(8,128)S(1)}, f32[3,128,256]{2,1,0:T(8,128)}, u32[]{:S(2)}) copy-start(f32[3,128,256]{2,1,0:T(8,128)} %refs_6_.1) | copy-start | bytes 1179652
  43.6 10.0 %copy-start.3 = (f32[3,256]{1,0:T(4,128)S(1)}, f32[3,256]{1,0:T(4,128)}, u32[]{:S(2)}) copy-start(f32[3,256]{1,0:T(4,128)} %refs_2_.9) | copy-start | bytes 9220
  43.7 10.0 %copy-start.4 = (f32[3,256]{1,0:T(4,128)S(1)}, f32[3,256]{1,0:T(4,128)}, u32[]{:S(2)}) copy-start(f32[3,256]{1,0:T(4,128)} %refs_3_.9) | copy-start | bytes 9220
  43.7 10.0 %copy-start.5 = (f32[3,256]{1,0:T(4,128)S(1)}, f32[3,256]{1,0:T(4,128)}, u32[]{:S(2)}) copy-start(f32[3,256]{1,0:T(4,128)} %refs_4_.9) | copy-start | bytes 9220
  43.7 10.0 %copy-start.6 = (f32[3,256]{1,0:T(4,128)S(1)}, f32[3,256]{1,0:T(4,128)}, u32[]{:S(2)}) copy-start(f32[3,256]{1,0:T(4,128)} %refs_5_.9) | copy-start | bytes 9220
  43.7 9.5 %collective-permute-start.4 = (bf16[5,3,96,128]{3,2,1,0:T(8,128)(2,1)S(1)}, bf16[5,3,96,128]{3,2,1,0:T(8,128)(2,1)S(1)}, u32[]{:S(2)}, u32[]{:S(2)}) collective-permute-start(bf16[5,3,96,128]{3,2,1,0:T(8,128)(2,1)S(1)} %get-tuple-element.40), channel_id=1, source_target_pairs={{0,1},{1,0},{2,3},{3,2},{4,5},{5,4},{6,7},{7,6},{8,9},{9,8},{10,11... | collective-permute-start | bytes 1105928 | tf_op jit(solution)/shard_map/ppermute | solution.py:255
  46.0 9.9 %collective-permute-start.5 = (bf16[5,3,96,128]{3,2,1,0:T(8,128)(2,1)S(1)}, bf16[5,3,96,128]{3,2,1,0:T(8,128)(2,1)S(1)}, u32[]{:S(2)}, u32[]{:S(2)}) collective-permute-start(bf16[5,3,96,128]{3,2,1,0:T(8,128)(2,1)S(1)} %get-tuple-element.42), channel_id=1, source_target_pairs={{2,4},{4,2},{6,8},{8,6},{10,12},{12,10},{14,16},{16,14},{18,20},{2... | collective-permute-start | bytes 1105928 | tf_op jit(solution)/shard_map/ppermute | solution.py:219
  50.0 9.6 %collective-permute-start.10 = (bf16[5,3,96,128]{3,2,1,0:T(8,128)(2,1)S(1)}, bf16[5,3,96,128]{3,2,1,0:T(8,128)(2,1)S(1)}, u32[]{:S(2)}, u32[]{:S(2)}) collective-permute-start(bf16[5,3,96,128]{3,2,1,0:T(8,128)(2,1)S(1)} %get-tuple-element.51), channel_id=1, source_target_pairs={{0,1},{1,0},{2,3},{3,2},{4,5},{5,4},{6,7},{7,6},{8,9},{9,8},{10,11... | collective-permute-start | bytes 1105928 | tf_op jit(solution)/shard_map/ppermute | solution.py:255
  51.4 8.2 %collective-permute-start.8 = (bf16[3,3,96,128]{3,2,1,0:T(8,128)(2,1)S(1)}, bf16[3,3,96,128]{3,2,1,0:T(8,128)(2,1)S(1)}, u32[]{:S(2)}, u32[]{:S(2)}) collective-permute-start(bf16[3,3,96,128]{3,2,1,0:T(8,128)(2,1)S(1)} %get-tuple-element.48), channel_id=1, source_target_pairs={{2,4},{4,2},{6,8},{8,6},{10,12},{12,10},{14,16},{16,14},{18,20},{2... | collective-permute-start | bytes 663560 | tf_op jit(solution)/shard_map/ppermute | solution.py:219
  53.2 8.1 %collective-permute-start.11 = (bf16[2,3,96,128]{3,2,1,0:T(8,128)(2,1)S(1)}, bf16[2,3,96,128]{3,2,1,0:T(8,128)(2,1)S(1)}, u32[]{:S(2)}, u32[]{:S(2)}) collective-permute-start(bf16[2,3,96,128]{3,2,1,0:T(8,128)(2,1)S(1)} %get-tuple-element.54), channel_id=1, source_target_pairs={{2,4},{4,2},{6,8},{8,6},{10,12},{12,10},{14,16},{16,14},{18,20},{2... | collective-permute-start | bytes 442376 | tf_op jit(solution)/shard_map/ppermute | solution.py:219
  55.9 6.0 %collective-permute-start.12 = (bf16[1,3,96,128]{3,2,1,0:T(8,128)(2,1)S(1)}, bf16[1,3,96,128]{3,2,1,0:T(8,128)(2,1)S(1)}, u32[]{:S(2)}, u32[]{:S(2)}) collective-permute-start(bf16[1,3,96,128]{3,2,1,0:T(8,128)(2,1)S(1)} %get-tuple-element.56), channel_id=1, source_target_pairs={{2,4},{4,2},{6,8},{8,6},{10,12},{12,10},{14,16},{16,14},{18,20},{2... | collective-permute-start | bytes 221192 | tf_op jit(solution)/shard_map/ppermute | solution.py:219
where the time goes:
time: 63.3 us; the launch traced here: 63.1 us
  waiting for transfers between devices  31.9 us (50%)
  starting transfers between devices  16 us (25%)
  Pallas kernels  12.1 us (19%)
  local copies, waits for them, and re-layouts  2.93 us (5%)
    ppermute x8, waiting for transfers between devices, shards(): lax.ppermute(x, 'gy', link_pairs)  31.9 us
    ppermute x8, starting transfers between devices, shards(): lax.ppermute(x, 'gy', link_pairs)  12.2 us
    pallas_call x5, Pallas kernels, shards(): pl.pallas_call(functools.partial(velocity_kernel, (s, n), [near_chunks[q]...  7.94 us
    ppermute x3, starting transfers between devices, shards(): near_halo = [lax.ppermute(edge, 'gz', near_pairs) for _, edge in near]  3.16 us
    pallas_call x3, Pallas kernels, smooth(): pl.pallas_call(functools.partial(smooth_kernel, start, block, 2), out_sha...  3.02 us
    unnamed x14, local copies, waits for them, and re-layouts  1.92 us
  transfers between devices with their start and end apart: 13, of which 3 were waited for; matrix products, arithmetic and copies ran while one was open for 0% of the time, Pallas kernels for 16%

commit v1 on v0

--- a/solution.py
+++ b/solution.py
@@ -27,7 +27,7 @@
 def chunks_of(steps):
     cut = lambda ends: [(a, b - a) for a, b in zip([0] + ends, ends)]
     sixteenths = lambda *parts: sorted({max(1, p * steps // 16) for p in parts})
-    return cut(sixteenths(5, 11, 16)), cut(sixteenths(5, 10, 13, 15, 16))
+    return cut(sixteenths(4, 10, 16)), cut(sixteenths(5, 10, 13, 15, 16))
 
 
 def parity(axis):
@@ -144,7 +144,7 @@
         copies.append(pltpu.make_async_copy(kept_ref, velocity.at[pl.ds(*kept)], sems.at[0]))
         copies[0].start()
 
-    parts, rows = own.shape[1:3]
+    parts, _ = own.shape[1:3]
     keep = decay[...]
     fresh = jnp.sqrt(1.0 - keep * keep)
     line = lambda x, c: x[c : c + 1, :]
@@ -164,9 +164,9 @@
                 row += [ref[step - sources[q], c].T for ref in near_halo[q : q + 1]]
                 row += [ref[t, c].T for ref in far_halo]
                 cells.append(jnp.concatenate(row, axis=1))
-            filtered = jnp.dot(jnp.concatenate(cells, axis=0), band, preferred_element_type=jnp.float32)
             for c in range(parts):
-                now[c] = line(keep, c) * now[c] + line(fresh, c) * filtered[c * rows : (c + 1) * rows]
+                filtered = jnp.dot(cells[c], band, preferred_element_type=jnp.float32)
+                now[c] = line(keep, c) * now[c] + line(fresh, c) * filtered
                 value = line(u, c) + line(d, c) * now[c]
                 for e in range(c):
                     value = value + line(o, (c * (c - 1)) // 2 + e) * now[e]
@@ -189,6 +189,7 @@
     wall_count = lax.axis_size("gz")
     kind = random_fields.dtype
     params = pltpu.CompilerParams(vmem_limit_bytes=GRANT)
+    tight = pltpu.CompilerParams(vmem_limit_bytes=GRANT)
 
     core_pairs = pairs(span_count, 0, True)
     link_pairs = pairs(span_count, 1, True)
@@ -240,7 +241,7 @@
             ),
             in_specs=[VMEM] * 4,
             out_specs=(VMEM, VMEM),
-            compiler_params=params,
+            compiler_params=tight,
             cost_estimate=pl.CostEstimate(
                 flops=2 * count * parts * rows * lanes * (rows + 2 * HALF),
                 bytes_accessed=4 * count * parts * lanes * (rows + HALF),
@@ -302,7 +303,7 @@
             out_specs=places,
             scratch_shapes=scratch,
             input_output_aliases=aliases,
-            compiler_params=params,
+            compiler_params=tight,
             cost_estimate=pl.CostEstimate(
                 flops=2 * n * parts * rows * (lanes * (rows + 2 * HALF) + cols * depth),
                 bytes_accessed=n * parts * rows * (4 * cols + 10 * lanes),

time: 63.3 us -> 67.7 us (1.070)
  waiting for transfers between devices: 31.9 us -> 38 us
  starting transfers between devices: 16 us -> 14.8 us
    ppermute x3, waiting for transfers between devices: 0.01 us -> 4.05 us  [shards(): near_halo = [lax.ppermute(edge, 'gz', near_pairs) for _, edge in near]]
    ppermute x8, waiting for transfers between devices: 31.9 us -> 34 us  [shards(): lax.ppermute(x, 'gy', link_pairs)]
    ppermute x8, starting transfers between devices: 12.2 us -> 10.3 us  [shards(): lax.ppermute(x, 'gy', link_pairs)]
    ppermute x3, starting transfers between devices: 3.16 us -> 3.94 us  [shards(): near_halo = [lax.ppermute(edge, 'gz', near_pairs) for _, edge in near]]
  transfers between devices with their start and end apart: 13 -> 13, of which waited for: 3 -> 4; matrix products, arithmetic and copies ran while one was open for 0% -> 0% of each run, Pallas kernels for 16% -> 14%
where the time goes in v1:
time: 67.7 us; the launch traced here: 67.5 us
  waiting for transfers between devices  38 us (56%)
  starting transfers between devices  14.8 us (22%)
  Pallas kernels  11.6 us (17%)
  local copies, waits for them, and re-layouts  2.9 us (4%)
    ppermute x8, waiting for transfers between devices, shards(): lax.ppermute(x, 'gy', link_pairs)  34 us
    ppermute x8, starting transfers between devices, shards(): lax.ppermute(x, 'gy', link_pairs)  10.3 us
    pallas_call x5, Pallas kernels, shards(): pl.pallas_call(functools.partial(velocity_kernel, (s, n), [near_chunks[q]...  7.61 us
    ppermute x3, waiting for transfers between devices, shards(): near_halo = [lax.ppermute(edge, 'gz', near_pairs) for _, edge in near]  4.05 us
    ppermute x3, starting transfers between devices, shards(): near_halo = [lax.ppermute(edge, 'gz', near_pairs) for _, edge in near]  3.94 us
    pallas_call x3, Pallas kernels, smooth(): pl.pallas_call(functools.partial(smooth_kernel, start, block, 2), out_sha...  2.84 us
    unnamed x14, local copies, waits for them, and re-layouts  1.92 us
  transfers between devices with their start and end apart: 13, of which 4 were waited for; matrix products, arithmetic and copies ran while one was open for 0% of the time, Pallas kernels for 14%

profile of v1, /device:TPU:1, one launch (start us, length us, event | category | flops | bytes accessed | tf_op | source)
XLA Modules:
  0.0 67.5 jit_solution(3999954368812349645)
XLA Ops:
  0.0 1.0 %constant_dynamic-slice_fusion = bf16[4,3,96,128]{3,2,1,0:T(8,128)(2,1)S(1)} fusion(bf16[16,3,128,256]{3,2,1,0:T(8,128)(2,1)} %refs_7_.4, s32[]{:T(128)S(6)} %select_n.18, s32[]{:T(128)S(6)} %select_n.20), kind=kLoop, calls=%fused_computation | loop fusion | bytes 589832 | tf_op jit(solution)/shard_map/dynamic_slice | solution.py:201
  1.0 0.0 copy-start
  1.0 1.9 %copy-done = bf16[16,3,128,256]{3,2,1,0:T(8,128)(2,1)S(1)} copy-done((bf16[16,3,128,256]{3,2,1,0:T(8,128)(2,1)S(1)}, bf16[16,3,128,256]{3,2,1,0:T(8,128)(2,1)}, u32[]{:S(2)}) %copy-start) | copy-done | bytes 3145752
  2.9 0.0 copy-start.1
  2.9 0.8 %pack.1 = (bf16[16,3,96,128]{3,2,1,0:T(8,128)(2,1)S(1)}, bf16[6,3,96,128]{3,2,1,0:T(8,128)(2,1)S(1)}, bf16[6,3,96,128]{3,2,1,0:T(8,128)(2,1)S(1)}, bf16[5,3,96,1...) custom-call(bf16[16,3,128,256]{3,2,1,0:T(8,128)(2,1)S(1)} %copy-done), custom_call_target="tpu_custom_call" | custom-call | tf_op jit(solution)/shard_map/pack/pallas_call | solution.py:210
  3.6 0.1 collective-permute-start.2
  3.7 0.5 collective-permute-start
  4.2 2.6 %collective-permute-start.4 = (bf16[6,3,96,128]{3,2,1,0:T(8,128)(2,1)S(1)}, bf16[6,3,96,128]{3,2,1,0:T(8,128)(2,1)S(1)}, u32[]{:S(2)}, u32[]{:S(2)}) collective-permute-start(bf16[6,3,96,128]{3,2,1,0:T(8,128)(2,1)S(1)} %get-tuple-element.40), channel_id=1, source_target_pairs={{2,4},{4,2},{6,8},{8,6},{10,12},{12,10},{14,16},{16,14},{18,20},{2... | collective-permute-start | bytes 1327112 | tf_op jit(solution)/shard_map/ppermute | solution.py:220
  6.8 0.0 collective-permute-start.9
  6.9 1.7 %collective-permute-start.1 = (bf16[5,3,96,128]{3,2,1,0:T(8,128)(2,1)S(1)}, bf16[5,3,96,128]{3,2,1,0:T(8,128)(2,1)S(1)}, u32[]{:S(2)}, u32[]{:S(2)}) collective-permute-start(bf16[5,3,96,128]{3,2,1,0:T(8,128)(2,1)S(1)} %get-tuple-element.36), channel_id=1, source_target_pairs={{2,4},{4,2},{6,8},{8,6},{10,12},{12,10},{14,16},{16,14},{18,20},{2... | collective-permute-start | bytes 1105928 | tf_op jit(solution)/shard_map/ppermute | solution.py:220
  8.6 21.1 %collective-permute-done.4.link = bf16[6,3,96,128]{3,2,1,0:T(8,128)(2,1)S(1)} collective-permute-done((bf16[6,3,96,128]{3,2,1,0:T(8,128)(2,1)S(1)}, bf16[6,3,96,128]{3,2,1,0:T(8,128)(2,1)S(1)}, u32[]{:S(2)}, u32[]{:S(2)}) %collective-permute-start.4) | collective-permute-done | bytes 442400 | tf_op jit(solution)/shard_map/ppermute | solution.py:220
  29.7 1.4 %collective-permute-start.3 = (bf16[4,3,96,128]{3,2,1,0:T(8,128)(2,1)S(1)}, bf16[4,3,96,128]{3,2,1,0:T(8,128)(2,1)S(1)}, u32[]{:S(2)}, u32[]{:S(2)}) collective-permute-start(bf16[4,3,96,128]{3,2,1,0:T(8,128)(2,1)S(1)} %constant_dynamic-slice_fusion), channel_id=1, source_target_pairs={{2,4},{4,2},{6,8},{8,6},{10,12},{12,10},{14,16},{16,14},{18,20},{2... | collective-permute-start | bytes 884744 | tf_op jit(solution)/shard_map/ppermute | solution.py:220
  31.2 0.4 bands.1
  31.5 0.0 collective-permute-done.2.core
  31.5 0.0 copy-done.1
  31.5 1.1 %smooth.4 = (bf16[6,3,128,128]{3,2,1,0:T(8,128)(2,1)S(1)}, bf16[6,3,96,128]{3,2,1,0:T(8,128)(2,1)S(1)}) custom-call(bf16[128,320]{1,0:T(8,128)(2,1)S(1)} %get-tuple-element.32.weights.refs_0_, bf16[16,3,128,256]{3,2,1,0:T(8,128)(2,1)S(1)} %copy-done.1, bf16[16,3,96,128]{3,2,1,0:T(8,128)(2,1)S(1)} %collective-permute-done.2.core, ...), custom_call_target="tpu_custom_call" | custom-call | flops 188743680 | bytes 2064384 | tf_op jit(solution)/shard_map/smooth/pallas_call | solution.py:236
  32.6 1.3 %collective-permute-start.6 = (bf16[6,3,96,128]{3,2,1,0:T(8,128)(2,1)S(1)}, bf16[6,3,96,128]{3,2,1,0:T(8,128)(2,1)S(1)}, u32[]{:S(2)}, u32[]{:S(2)}) collective-permute-start(bf16[6,3,96,128]{3,2,1,0:T(8,128)(2,1)S(1)} %get-tuple-element.43), channel_id=1, source_target_pairs={{0,1},{1,0},{2,3},{3,2},{4,5},{5,4},{6,7},{7,6},{8,9},{9,8},{10,11... | collective-permute-start | bytes 1327112 | tf_op jit(solution)/shard_map/ppermute | solution.py:256
  33.9 8.2 %collective-permute-done.9.link = bf16[6,3,96,128]{3,2,1,0:T(8,128)(2,1)S(1)} collective-permute-done((bf16[6,3,96,128]{3,2,1,0:T(8,128)(2,1)S(1)}, bf16[6,3,96,128]{3,2,1,0:T(8,128)(2,1)S(1)}, u32[]{:S(2)}, u32[]{:S(2)}) %collective-permute-start.9) | collective-permute-done | bytes 442400 | tf_op jit(solution)/shard_map/ppermute | solution.py:220
  42.1 1.1 %smooth.5 = (bf16[6,3,128,128]{3,2,1,0:T(8,128)(2,1)S(1)}, bf16[6,3,96,128]{3,2,1,0:T(8,128)(2,1)S(1)}) custom-call(bf16[128,320]{1,0:T(8,128)(2,1)S(1)} %get-tuple-element.32.weights.refs_0_, bf16[16,3,128,256]{3,2,1,0:T(8,128)(2,1)S(1)} %copy-done.1, bf16[16,3,96,128]{3,2,1,0:T(8,128)(2,1)S(1)} %collective-permute-done.2.core, ...), custom_call_target="tpu_custom_call" | custom-call | flops 188743680 | bytes 2064384 | tf_op jit(solution)/shard_map/smooth/pallas_call | solution.py:236
  43.2 0.0 copy-start.2
  43.2 0.0 copy-start.3
  43.2 0.0 copy-start.4
  43.2 0.0 copy-start.5
  43.2 0.0 copy-start.6
  43.2 1.3 %collective-permute-start.10 = (bf16[6,3,96,128]{3,2,1,0:T(8,128)(2,1)S(1)}, bf16[6,3,96,128]{3,2,1,0:T(8,128)(2,1)S(1)}, u32[]{:S(2)}, u32[]{:S(2)}) collective-permute-start(bf16[6,3,96,128]{3,2,1,0:T(8,128)(2,1)S(1)} %get-tuple-element.51), channel_id=1, source_target_pairs={{0,1},{1,0},{2,3},{3,2},{4,5},{5,4},{6,7},{7,6},{8,9},{9,8},{10,11... | collective-permute-start | bytes 1327112 | tf_op jit(solution)/shard_map/ppermute | solution.py:256
  44.6 4.7 %collective-permute-done.3.link = bf16[4,3,96,128]{3,2,1,0:T(8,128)(2,1)S(1)} collective-permute-done((bf16[4,3,96,128]{3,2,1,0:T(8,128)(2,1)S(1)}, bf16[4,3,96,128]{3,2,1,0:T(8,128)(2,1)S(1)}, u32[]{:S(2)}, u32[]{:S(2)}) %collective-permute-start.3) | collective-permute-done | bytes 294944 | tf_op jit(solution)/shard_map/ppermute | solution.py:220
  49.2 2.5 %collective-permute-start.7 = (bf16[5,3,96,128]{3,2,1,0:T(8,128)(2,1)S(1)}, bf16[5,3,96,128]{3,2,1,0:T(8,128)(2,1)S(1)}, u32[]{:S(2)}, u32[]{:S(2)}) collective-permute-start(bf16[5,3,96,128]{3,2,1,0:T(8,128)(2,1)S(1)} %get-tuple-element.45), channel_id=1, source_target_pairs={{2,4},{4,2},{6,8},{8,6},{10,12},{12,10},{14,16},{16,14},{18,20},{2... | collective-permute-start | bytes 1105928 | tf_op jit(solution)/shard_map/ppermute | solution.py:220
  51.7 0.7 %smooth.3 = (bf16[4,3,128,128]{3,2,1,0:T(8,128)(2,1)S(1)}, bf16[4,3,96,128]{3,2,1,0:T(8,128)(2,1)S(1)}) custom-call(bf16[128,320]{1,0:T(8,128)(2,1)S(1)} %get-tuple-element.32.weights.refs_0_, bf16[16,3,128,256]{3,2,1,0:T(8,128)(2,1)S(1)} %copy-done.1, bf16[16,3,96,128]{3,2,1,0:T(8,128)(2,1)S(1)} %collective-permute-done.2.core, ...), custom_call_target="tpu_custom_call" | custom-call | flops 125829120 | bytes 1376256 | tf_op jit(solution)/shard_map/smooth/pallas_call | solution.py:236
  52.4 0.0 collective-permute-done.1.refs_9_
  52.4 1.3 %collective-permute-start.5 = (bf16[4,3,96,128]{3,2,1,0:T(8,128)(2,1)S(1)}, bf16[4,3,96,128]{3,2,1,0:T(8,128)(2,1)S(1)}, u32[]{:S(2)}, u32[]{:S(2)}) collective-permute-start(bf16[4,3,96,128]{3,2,1,0:T(8,128)(2,1)S(1)} %get-tuple-element.42), channel_id=1, source_target_pairs={{0,1},{1,0},{2,3},{3,2},{4,5},{5,4},{6,7},{7,6},{8,9},{9,8},{10,11... | collective-permute-start | bytes 884744 | tf_op jit(solution)/shard_map/ppermute | solution.py:256
  53.7 0.0 collective-permute-done.refs_8_
  53.7 0.3 collective-permute-start.8
  54.0 4.0 %collective-permute-done.5.refs_12_ = bf16[4,3,96,128]{3,2,1,0:T(8,128)(2,1)S(1)} collective-permute-done((bf16[4,3,96,128]{3,2,1,0:T(8,128)(2,1)S(1)}, bf16[4,3,96,128]{3,2,1,0:T(8,128)(2,1)S(1)}, u32[]{:S(2)}, u32[]{:S(2)}) %collective-permute-start.5) | collective-permute-done | bytes 294944 | tf_op jit(solution)/shard_map/ppermute | solution.py:256
  58.1 1.2 %collective-permute-start.11 = (bf16[2,3,96,128]{3,2,1,0:T(8,128)(2,1)S(1)}, bf16[2,3,96,128]{3,2,1,0:T(8,128)(2,1)S(1)}, u32[]{:S(2)}, u32[]{:S(2)}) collective-permute-start(bf16[2,3,96,128]{3,2,1,0:T(8,128)(2,1)S(1)} %get-tuple-element.54), channel_id=1, source_target_pairs={{2,4},{4,2},{6,8},{8,6},{10,12},{12,10},{14,16},{16,14},{18,20},{2... | collective-permute-start | bytes 442376 | tf_op jit(solution)/shard_map/ppermute | solution.py:220
  59.2 0.0 collective-permute-done.6.refs_13_.refs_11_
  59.2 0.6 collective-permute-start.12
  59.8 0.0 copy-done.2
  59.8 0.0 copy-done.3
  59.8 0.0 copy-done.4
  59.8 0.0 copy-done.5
  59.8 0.0 copy-done.6
  59.9 2.1 %velocity.5 = (f32[16,3,128,256]{3,2,1,0:T(8,128)}, f32[3,128,256]{2,1,0:T(8,128)S(1)}) custom-call(bf16[128,320]{1,0:T(8,128)(2,1)S(1)} %get-tuple-element.32.weights.refs_0_, bf16[352,256]{1,0:T(8,128)(2,1)S(1)} %get-tuple-element.33.refs_1_, f32[3,256]{1,0:T(4,128)S(1)} %copy-done.3, f32[3,256]{1,0:T(4,128)S(1)} %copy-done.4, f32[3,256]{1,0:T(4,128)S(1)} %copy-done.5, ...), custom_call_target="tpu_custom_call" | custom-call | flops 503316480 | bytes 4423680 | tf_op jit(solution)/shard_map/velocity/pallas_call | solution.py:290
  62.0 0.0 collective-permute-done.7.refs_9_
  62.0 2.1 %velocity.6 = (f32[16,3,128,256]{3,2,1,0:T(8,128)}, f32[3,128,256]{2,1,0:T(8,128)S(1)}) custom-call(bf16[128,320]{1,0:T(8,128)(2,1)S(1)} %get-tuple-element.32.weights.refs_0_, bf16[352,256]{1,0:T(8,128)(2,1)S(1)} %get-tuple-element.33.refs_1_, f32[3,256]{1,0:T(4,128)S(1)} %copy-done.3, f32[3,256]{1,0:T(4,128)S(1)} %copy-done.4, ...), custom_call_target="tpu_custom_call", output_to_operand_aliasing={{0}: (12, {})} | custom-call | flops 503316480 | bytes 4423680 | tf_op jit(solution)/shard_map/velocity/pallas_call | solution.py:290
  64.1 0.0 collective-permute-done.8.refs_9_
  64.1 0.0 collective-permute-done.10.refs_11_
  64.1 1.6 %velocity.7 = (f32[16,3,128,256]{3,2,1,0:T(8,128)}, f32[3,128,256]{2,1,0:T(8,128)S(1)}) custom-call(bf16[128,320]{1,0:T(8,128)(2,1)S(1)} %get-tuple-element.32.weights.refs_0_, bf16[352,256]{1,0:T(8,128)(2,1)S(1)} %get-tuple-element.33.refs_1_, f32[3,256]{1,0:T(4,128)S(1)} %copy-done.3, f32[3,256]{1,0:T(4,128)S(1)} %copy-done.4, ...), custom_call_target="tpu_custom_call", output_to_operand_aliasing={{0}: (12, {})} | custom-call | flops 301989888 | bytes 2654208 | tf_op jit(solution)/shard_map/velocity/pallas_call | solution.py:290
  65.8 0.0 collective-permute-done.11.refs_9_
  65.8 0.5 velocity.8
  66.3 0.0 collective-permute-done.12.refs_9_
  66.3 1.2 %velocity.9 = f32[16,3,128,256]{3,2,1,0:T(8,128)} custom-call(bf16[128,320]{1,0:T(8,128)(2,1)S(1)} %get-tuple-element.32.weights.refs_0_, bf16[352,256]{1,0:T(8,128)(2,1)S(1)} %get-tuple-element.33.refs_1_, f32[3,256]{1,0:T(4,128)S(1)} %copy-done.3, f32[3,256]{1,0:T(4,128)S(1)} %copy-done.4, ...), custom_call_target="tpu_custom_call", output_to_operand_aliasing={{}: (13, {})} | custom-call | flops 100663296 | bytes 884736 | tf_op jit(solution)/shard_map/velocity/pallas_call | solution.py:290
Async XLA Ops:
  1.0 1.9 %copy-start = (bf16[16,3,128,256]{3,2,1,0:T(8,128)(2,1)S(1)}, bf16[16,3,128,256]{3,2,1,0:T(8,128)(2,1)}, u32[]{:S(2)}) copy-start(bf16[16,3,128,256]{3,2,1,0:T(8,128)(2,1)} %refs_7_.4) | copy-start | bytes 9437188
  2.9 28.7 %copy-start.1 = (bf16[16,3,128,256]{3,2,1,0:T(8,128)(2,1)S(1)}, bf16[16,3,128,256]{3,2,1,0:T(8,128)(2,1)}, u32[]{:S(2)}) copy-start(bf16[16,3,128,256]{3,2,1,0:T(8,128)(2,1)} %refs_7_.4) | copy-start | bytes 9437188
  3.6 27.9 %collective-permute-start.2 = (bf16[16,3,96,128]{3,2,1,0:T(8,128)(2,1)S(1)}, bf16[16,3,96,128]{3,2,1,0:T(8,128)(2,1)S(1)}, u32[]{:S(2)}, u32[]{:S(2)}) collective-permute-start(bf16[16,3,96,128]{3,2,1,0:T(8,128)(2,1)S(1)} %get-tuple-element.37), channel_id=1, source_target_pairs={{0,2},{2,0},{4,6},{6,4},{8,10},{10,8},{12,14},{14,12},{16,18},{18,... | collective-permute-start | bytes 3538952 | tf_op jit(solution)/shard_map/ppermute | solution.py:218
  3.7 50.0 %collective-permute-start = (bf16[16,3,96,128]{3,2,1,0:T(8,128)(2,1)S(1)}, bf16[16,3,96,128]{3,2,1,0:T(8,128)(2,1)S(1)}, u32[]{:S(2)}, u32[]{:S(2)}) collective-permute-start(bf16[16,3,96,128]{3,2,1,0:T(8,128)(2,1)S(1)} %get-tuple-element.35), channel_id=1, source_target_pairs={{0,2},{2,0},{4,6},{6,4},{8,10},{10,8},{12,14},{14,12},{16,18},{18,... | collective-permute-start | bytes 3538952 | tf_op jit(solution)/shard_map/ppermute | solution.py:219
  4.2 25.5 %collective-permute-start.4 = (bf16[6,3,96,128]{3,2,1,0:T(8,128)(2,1)S(1)}, bf16[6,3,96,128]{3,2,1,0:T(8,128)(2,1)S(1)}, u32[]{:S(2)}, u32[]{:S(2)}) collective-permute-start(bf16[6,3,96,128]{3,2,1,0:T(8,128)(2,1)S(1)} %get-tuple-element.40), channel_id=1, source_target_pairs={{2,4},{4,2},{6,8},{8,6},{10,12},{12,10},{14,16},{16,14},{18,20},{2... | collective-permute-start | bytes 1327112 | tf_op jit(solution)/shard_map/ppermute | solution.py:220
  6.8 35.3 %collective-permute-start.9 = (bf16[6,3,96,128]{3,2,1,0:T(8,128)(2,1)S(1)}, bf16[6,3,96,128]{3,2,1,0:T(8,128)(2,1)S(1)}, u32[]{:S(2)}, u32[]{:S(2)}) collective-permute-start(bf16[6,3,96,128]{3,2,1,0:T(8,128)(2,1)S(1)} %get-tuple-element.49), channel_id=1, source_target_pairs={{2,4},{4,2},{6,8},{8,6},{10,12},{12,10},{14,16},{16,14},{18,20},{2... | collective-permute-start | bytes 1327112 | tf_op jit(solution)/shard_map/ppermute | solution.py:220
  6.9 45.6 %collective-permute-start.1 = (bf16[5,3,96,128]{3,2,1,0:T(8,128)(2,1)S(1)}, bf16[5,3,96,128]{3,2,1,0:T(8,128)(2,1)S(1)}, u32[]{:S(2)}, u32[]{:S(2)}) collective-permute-start(bf16[5,3,96,128]{3,2,1,0:T(8,128)(2,1)S(1)} %get-tuple-element.36), channel_id=1, source_target_pairs={{2,4},{4,2},{6,8},{8,6},{10,12},{12,10},{14,16},{16,14},{18,20},{2... | collective-permute-start | bytes 1105928 | tf_op jit(solution)/shard_map/ppermute | solution.py:220
  29.7 19.5 %collective-permute-start.3 = (bf16[4,3,96,128]{3,2,1,0:T(8,128)(2,1)S(1)}, bf16[4,3,96,128]{3,2,1,0:T(8,128)(2,1)S(1)}, u32[]{:S(2)}, u32[]{:S(2)}) collective-permute-start(bf16[4,3,96,128]{3,2,1,0:T(8,128)(2,1)S(1)} %constant_dynamic-slice_fusion), channel_id=1, source_target_pairs={{2,4},{4,2},{6,8},{8,6},{10,12},{12,10},{14,16},{16,14},{18,20},{2... | collective-permute-start | bytes 884744 | tf_op jit(solution)/shard_map/ppermute | solution.py:220
  32.6 26.6 %collective-permute-start.6 = (bf16[6,3,96,128]{3,2,1,0:T(8,128)(2,1)S(1)}, bf16[6,3,96,128]{3,2,1,0:T(8,128)(2,1)S(1)}, u32[]{:S(2)}, u32[]{:S(2)}) collective-permute-start(bf16[6,3,96,128]{3,2,1,0:T(8,128)(2,1)S(1)} %get-tuple-element.43), channel_id=1, source_target_pairs={{0,1},{1,0},{2,3},{3,2},{4,5},{5,4},{6,7},{7,6},{8,9},{9,8},{10,11... | collective-permute-start | bytes 1327112 | tf_op jit(solution)/shard_map/ppermute | solution.py:256
  43.2 16.7 %copy-start.2 = (f32[3,128,256]{2,1,0:T(8,128)S(1)}, f32[3,128,256]{2,1,0:T(8,128)}, u32[]{:S(2)}) copy-start(f32[3,128,256]{2,1,0:T(8,128)} %refs_6_.1) | copy-start | bytes 1179652
  43.2 16.7 %copy-start.3 = (f32[3,256]{1,0:T(4,128)S(1)}, f32[3,256]{1,0:T(4,128)}, u32[]{:S(2)}) copy-start(f32[3,256]{1,0:T(4,128)} %refs_2_.9) | copy-start | bytes 9220
  43.2 16.6 %copy-start.4 = (f32[3,256]{1,0:T(4,128)S(1)}, f32[3,256]{1,0:T(4,128)}, u32[]{:S(2)}) copy-start(f32[3,256]{1,0:T(4,128)} %refs_3_.9) | copy-start | bytes 9220
  43.2 16.6 %copy-start.5 = (f32[3,256]{1,0:T(4,128)S(1)}, f32[3,256]{1,0:T(4,128)}, u32[]{:S(2)}) copy-start(f32[3,256]{1,0:T(4,128)} %refs_4_.9) | copy-start | bytes 9220
  43.2 16.6 %copy-start.6 = (f32[3,256]{1,0:T(4,128)S(1)}, f32[3,256]{1,0:T(4,128)}, u32[]{:S(2)}) copy-start(f32[3,256]{1,0:T(4,128)} %refs_5_.9) | copy-start | bytes 9220
  43.2 20.9 %collective-permute-start.10 = (bf16[6,3,96,128]{3,2,1,0:T(8,128)(2,1)S(1)}, bf16[6,3,96,128]{3,2,1,0:T(8,128)(2,1)S(1)}, u32[]{:S(2)}, u32[]{:S(2)}) collective-permute-start(bf16[6,3,96,128]{3,2,1,0:T(8,128)(2,1)S(1)} %get-tuple-element.51), channel_id=1, source_target_pairs={{0,1},{1,0},{2,3},{3,2},{4,5},{5,4},{6,7},{7,6},{8,9},{9,8},{10,11... | collective-permute-start | bytes 1327112 | tf_op jit(solution)/shard_map/ppermute | solution.py:256
  49.2 12.8 %collective-permute-start.7 = (bf16[5,3,96,128]{3,2,1,0:T(8,128)(2,1)S(1)}, bf16[5,3,96,128]{3,2,1,0:T(8,128)(2,1)S(1)}, u32[]{:S(2)}, u32[]{:S(2)}) collective-permute-start(bf16[5,3,96,128]{3,2,1,0:T(8,128)(2,1)S(1)} %get-tuple-element.45), channel_id=1, source_target_pairs={{2,4},{4,2},{6,8},{8,6},{10,12},{12,10},{14,16},{16,14},{18,20},{2... | collective-permute-start | bytes 1105928 | tf_op jit(solution)/shard_map/ppermute | solution.py:220
  52.4 5.6 %collective-permute-start.5 = (bf16[4,3,96,128]{3,2,1,0:T(8,128)(2,1)S(1)}, bf16[4,3,96,128]{3,2,1,0:T(8,128)(2,1)S(1)}, u32[]{:S(2)}, u32[]{:S(2)}) collective-permute-start(bf16[4,3,96,128]{3,2,1,0:T(8,128)(2,1)S(1)} %get-tuple-element.42), channel_id=1, source_target_pairs={{0,1},{1,0},{2,3},{3,2},{4,5},{5,4},{6,7},{7,6},{8,9},{9,8},{10,11... | collective-permute-start | bytes 884744 | tf_op jit(solution)/shard_map/ppermute | solution.py:256
  53.7 10.4 %collective-permute-start.8 = (bf16[3,3,96,128]{3,2,1,0:T(8,128)(2,1)S(1)}, bf16[3,3,96,128]{3,2,1,0:T(8,128)(2,1)S(1)}, u32[]{:S(2)}, u32[]{:S(2)}) collective-permute-start(bf16[3,3,96,128]{3,2,1,0:T(8,128)(2,1)S(1)} %get-tuple-element.48), channel_id=1, source_target_pairs={{2,4},{4,2},{6,8},{8,6},{10,12},{12,10},{14,16},{16,14},{18,20},{2... | collective-permute-start | bytes 663560 | tf_op jit(solution)/shard_map/ppermute | solution.py:220
  58.1 7.7 %collective-permute-start.11 = (bf16[2,3,96,128]{3,2,1,0:T(8,128)(2,1)S(1)}, bf16[2,3,96,128]{3,2,1,0:T(8,128)(2,1)S(1)}, u32[]{:S(2)}, u32[]{:S(2)}) collective-permute-start(bf16[2,3,96,128]{3,2,1,0:T(8,128)(2,1)S(1)} %get-tuple-element.54), channel_id=1, source_target_pairs={{2,4},{4,2},{6,8},{8,6},{10,12},{12,10},{14,16},{16,14},{18,20},{2... | collective-permute-start | bytes 442376 | tf_op jit(solution)/shard_map/ppermute | solution.py:220
  59.2 7.1 %collective-permute-start.12 = (bf16[1,3,96,128]{3,2,1,0:T(8,128)(2,1)S(1)}, bf16[1,3,96,128]{3,2,1,0:T(8,128)(2,1)S(1)}, u32[]{:S(2)}, u32[]{:S(2)}) collective-permute-start(bf16[1,3,96,128]{3,2,1,0:T(8,128)(2,1)S(1)} %get-tuple-element.56), channel_id=1, source_target_pairs={{2,4},{4,2},{6,8},{8,6},{10,12},{12,10},{14,16},{16,14},{18,20},{2... | collective-permute-start | bytes 221192 | tf_op jit(solution)/shard_map/ppermute | solution.py:220
